TPU v7x, 16 devices: a 4x2x1 block of a 4x4x8 slice. The times are simulated.
16 devices in a mesh: rep: 4 (over y, z, core), pp: 4 (over x).
Axes of the slice: x: 4, y: 2, z: 1, core: 2. Of those that a mesh axis runs over, the one named last changes fastest.
The devices are a block of a 4x4x8 slice.
Arguments:
- x: bfloat16 [32, 512, 640], P('rep'), parts along dimension 0
- dy: bfloat16 [32, 512, 640], P('rep'), parts along dimension 0
- w_gate: bfloat16 [4, 640, 1536], P('pp')
- w_up: bfloat16 [4, 640, 1536], P('pp')
- w_down: bfloat16 [4, 1536, 640], P('pp')
Outputs:
- output 1: bfloat16 [16, 640, 1536], P(('rep', 'pp')), parts along dimension 0
- output 2: bfloat16 [16, 640, 1536], P(('rep', 'pp')), parts along dimension 0
- output 3: bfloat16 [16, 1536, 640], P(('rep', 'pp')), parts along dimension 0
There are 4 independent parts. A program takes and returns all parts, laid end to end along the dimension named above; an argument that names none is the same for every part.
All inputs are finite; a program needn't handle non-finite values.
Results may differ from a plain program's by a relative error of at most 0.018.
Values are sent between devices in bfloat16 or wider.
A program may use at most 768 MiB of HBM per device.

v0:
```python
import functools

import jax
import jax.numpy as jnp
from jax import lax
from jax.experimental import pallas as pl
from jax.experimental.pallas import tpu as pltpu
from jax.sharding import PartitionSpec as P

MESH = pl.DeviceIdType.MESH
CHUNK = 128
BLOCK = 512
LAG = 4
SLOTS = 4

f32, bf16 = jnp.float32, jnp.bfloat16


def dot(a, b):
    return jnp.dot(a, b, preferred_element_type=f32)


def norm_of(h):
    wide = h.astype(f32)
    return wide, lax.rsqrt(jnp.mean(wide * wide, -1, keepdims=True) + 1e-6)


def kernel(stages, micro, tokens, x, dy, wg_in, wu_in, wd_in, og, ou, od, wg, wu, wd, wgt, wut, wdt, sum_g, sum_u, sum_d, h_in, g_in,
           h_out, g_out, kept_g, kept_u, mid, act, dgate, dup, at, load_sem, h_recv, g_recv, h_send, g_send):
    me = lax.axis_index("pp")
    c, per = CHUNK, tokens // CHUNK
    chunks = micro * per
    ff, d = wd.shape
    ring = kept_g.shape[0]
    lag = (stages - 1 - me) * LAG
    first, last = me == 0, me == stages - 1

    loads = [pltpu.make_async_copy(src, dst, load_sem.at[n]) for n, (src, dst) in enumerate(((wg_in, wg), (wu_in, wu), (wd_in, wd)))]
    for load in loads:
        load.start()

    def rows(i):
        return pl.ds(pl.multiple_of(i * c, c), c)

    def fetch(src, dst, sem):
        def one(i, carry):
            pltpu.make_async_copy(src.at[rows(i), :], dst.at[rows(i), :], sem.at[i]).start()
            return carry
        lax.fori_loop(0, chunks, one, 0)

    @pl.when(first)
    def _():
        fetch(x, h_in, h_recv)

    @pl.when(last)
    def _():
        fetch(dy, g_in, g_recv)

    barrier = pltpu.get_barrier_semaphore()

    @pl.when(me > 0)
    def _():
        pl.semaphore_signal(barrier, inc=1, device_id={"pp": me - 1}, device_id_type=MESH)

    @pl.when(me < stages - 1)
    def _():
        pl.semaphore_signal(barrier, inc=1, device_id={"pp": me + 1}, device_id_type=MESH)

    pl.semaphore_wait(barrier, (me > 0).astype(jnp.int32) + (me < stages - 1).astype(jnp.int32))
    for load in loads:
        load.wait()

    def transposes():
        for n in range(0, ff, 256):
            s = slice(n, n + 256)
            wgt[s, :] = wg[:, s].T
            wut[s, :] = wu[:, s].T
            wdt[:, s] = wd[s, :].T

    def h_copy(i):
        return pltpu.make_async_remote_copy(
            src_ref=h_out.at[lax.rem(i, SLOTS)], dst_ref=h_in.at[rows(i), :], send_sem=h_send.at[lax.rem(i, SLOTS)], recv_sem=h_recv.at[i],
            device_id={"pp": me + 1}, device_id_type=MESH)

    def g_copy(i):
        return pltpu.make_async_remote_copy(
            src_ref=g_out.at[lax.rem(i, SLOTS)], dst_ref=g_in.at[rows(i), :], send_sem=g_send.at[lax.rem(i, SLOTS)], recv_sem=g_recv.at[i],
            device_id={"pp": me - 1}, device_id_type=MESH)

    def forward(i):
        pltpu.make_async_copy(h_in.at[rows(i), :], h_in.at[rows(i), :], h_recv.at[i]).wait()
        wide, scale = norm_of(h_in[rows(i), :])
        a = (wide * scale).astype(bf16)
        slot = lax.rem(i, ring)
        for n in range(0, ff, BLOCK):
            s = slice(n, n + BLOCK)
            gate, up = dot(a, wg[:, s]), dot(a, wu[:, s])
            kept_g[slot, :, s] = gate
            kept_u[slot, :, s] = up
            mid[:, s] = (gate * jax.nn.sigmoid(gate) * up).astype(bf16)

        @pl.when(me < stages - 1)
        def _():
            @pl.when(i >= SLOTS)
            def _():
                h_copy(i - SLOTS).wait_send()

            m = dot(mid[...], wd[...]).astype(bf16)
            h_out[lax.rem(i, SLOTS)] = (h_in[rows(i), :].astype(f32) + m.astype(f32)).astype(bf16)
            h_copy(i).start()

    def backward(i):
        pltpu.make_async_copy(g_in.at[rows(i), :], g_in.at[rows(i), :], g_recv.at[i]).wait()
        slot = lax.rem(i, ring)
        place = lax.rem(i, 2 * per)
        here = pl.ds(pl.multiple_of(place * c, c), c)

        @pl.when(first)
        def _():
            wide, scale = norm_of(h_in[rows(i), :])
            a = (wide * scale).astype(bf16)
            for n in range(0, ff, BLOCK):
                s = slice(n, n + BLOCK)
                kept_g[slot, :, s] = dot(a, wg[:, s])
                kept_u[slot, :, s] = dot(a, wu[:, s])

        g = g_in[rows(i), :]
        for n in range(0, ff, BLOCK):
            s = slice(n, n + BLOCK)
            by_act = dot(g, wdt[:, s]).astype(bf16).astype(f32)
            gate, up = kept_g[slot, :, s], kept_u[slot, :, s]
            part = jax.nn.sigmoid(gate)
            silu = gate * part
            act[here, s] = (silu * up).astype(bf16)
            dup[here, s] = (by_act * silu).astype(bf16)
            dgate[here, s] = (by_act * up * (part + silu * (1.0 - part))).astype(bf16)

        @pl.when(me > 0)
        def _():
            @pl.when(i >= SLOTS)
            def _():
                g_copy(i - SLOTS).wait_send()

            by_a = dot(dgate[here, :], wgt[...]).astype(bf16).astype(f32) + dot(dup[here, :], wut[...]).astype(bf16).astype(f32)
            by_a = by_a.astype(bf16).astype(f32)
            wide, scale = norm_of(h_in[rows(i), :])
            by_scale = jnp.sum(by_a * wide, -1, keepdims=True)
            by_h = by_a * scale - wide * (by_scale * scale * scale * scale * (1.0 / d))
            g_out[lax.rem(i, SLOTS)] = (g_in[rows(i), :].astype(f32) + by_h.astype(bf16).astype(f32)).astype(bf16)
            g_copy(i).start()

    def weights(m, q):
        half = pl.ds(pl.multiple_of(lax.rem(m, 2) * tokens, tokens), tokens)
        whole = pl.ds(pl.multiple_of(m * tokens, tokens), tokens)

        @pl.when(q == 0)
        def _():
            wide, scale = norm_of(h_in[whole, :])
            at[...] = (wide * scale).astype(bf16).T

        def add(total, here, s, left, right):
            term = dot(left, right).astype(bf16).astype(f32)
            total[here, s] = jnp.where(m == 0, 0.0, total[here, s]) + term

        part = d // per
        here = pl.ds(pl.multiple_of(q * part, part), part)
        left = at[here, :]
        for n in range(0, ff, BLOCK):
            s = slice(n, n + BLOCK)
            add(sum_g, here, s, left, dgate[half, s])
            add(sum_u, here, s, left, dup[half, s])
        part = ff // per
        here = pl.ds(pl.multiple_of(q * part, part), part)
        left = act[half, here].T
        add(sum_d, here, slice(None), left, g_in[whole, :])

    def step(t, carry):
        @pl.when(t < chunks)
        def _():
            forward(t)

        @pl.when(t == jnp.where(first, SLOTS - 1, 0))
        def _():
            transposes()

        j = t - lag

        @pl.when((j >= 0) & (j < chunks))
        def _():
            backward(j)

        @pl.when(j >= per)
        def _():
            weights(j // per - 1, lax.rem(j, per))
        return carry

    lax.fori_loop(0, lag + chunks + per, step, 0)

    for i in range(chunks - SLOTS, chunks):
        @pl.when(me < stages - 1)
        def _():
            h_copy(i).wait_send()

        @pl.when(me > 0)
        def _():
            g_copy(i).wait_send()

    stores = []
    for n, (total, staged, out) in enumerate(((sum_g, dgate.at[pl.ds(0, d), :], og), (sum_u, dup.at[pl.ds(0, d), :], ou), (sum_d, h_in.at[pl.ds(0, ff), :], od))):
        staged[...] = total[...].astype(bf16)
        stores.append(pltpu.make_async_copy(staged, out, load_sem.at[n]))
        stores[-1].start()
    for store in stores:
        store.wait()


def solution(mesh):
    stages = mesh.shape["pp"]

    def step(x, dy, w_gate, w_up, w_down):
        micro, tokens, d = x.shape
        ff = w_gate.shape[-1]
        chunks = micro * tokens // CHUNK
        ring = (stages - 2) * LAG + 1
        hbm = pl.BlockSpec(memory_space=pl.ANY)
        dma = pltpu.SemaphoreType.DMA
        outs = pl.pallas_call(
            functools.partial(kernel, stages, micro, tokens),
            out_shape=[jax.ShapeDtypeStruct(w.shape[1:], bf16) for w in (w_gate, w_up, w_down)],
            in_specs=[hbm] * 5,
            out_specs=[hbm] * 3,
            scratch_shapes=[
                pltpu.VMEM((d, ff), bf16), pltpu.VMEM((d, ff), bf16), pltpu.VMEM((ff, d), bf16),
                pltpu.VMEM((ff, d), bf16), pltpu.VMEM((ff, d), bf16), pltpu.VMEM((d, ff), bf16),
                pltpu.VMEM((d, ff), f32), pltpu.VMEM((d, ff), f32), pltpu.VMEM((ff, d), f32),
                pltpu.VMEM((micro * tokens, d), bf16), pltpu.VMEM((micro * tokens, d), bf16),
                pltpu.VMEM((SLOTS, CHUNK, d), bf16), pltpu.VMEM((SLOTS, CHUNK, d), bf16),
                pltpu.VMEM((ring, CHUNK, ff), f32), pltpu.VMEM((ring, CHUNK, ff), f32),
                pltpu.VMEM((CHUNK, ff), bf16),
                pltpu.VMEM((2 * tokens, ff), bf16), pltpu.VMEM((2 * tokens, ff), bf16), pltpu.VMEM((2 * tokens, ff), bf16),
                pltpu.VMEM((d, tokens), bf16),
                dma((3,)), dma((chunks,)), dma((chunks,)), dma((SLOTS,)), dma((SLOTS,)),
            ],
            compiler_params=pltpu.CompilerParams(collective_id=0, has_side_effects=True, vmem_limit_bytes=67043328),
        )(x.reshape(micro * tokens, d), dy.reshape(micro * tokens, d), w_gate[0], w_up[0], w_down[0])
        return tuple(out[None] for out in outs)

    return jax.shard_map(
        step,
        mesh=mesh,
        in_specs=(P("rep", None, None),) * 2 + (P("pp", None, None),) * 3,
        out_specs=(P(("rep", "pp"), None, None),) * 3,
        check_vma=False,
    )
```

profile of v0, /device:TPU:120, one launch (start us, length us, event | category | flops | bytes accessed | tf_op | source)
XLA Modules:
  0.0 182.1 jit_solution(7661628100625536023)
XLA Ops:
  0.6 174.8 %shard_map.76 = (bf16[640,1536]{1,0:T(8,128)(2,1)}, bf16[640,1536]{1,0:T(8,128)(2,1)}, bf16[1536,640]{1,0:T(8,128)(2,1)}) custom-call(bf16[4096,640]{1,0:T(8,128)(2,1)} %bitcast.8, bf16[4096,640]{1,0:T(8,128)(2,1)} %bitcast.9, bf16[640,1536]{1,0:T(8,128)(2,1)} %bitcast.13, bf16[640,1536]{1,0:T(8,128)(2,1)} %bitcast.14, bf16[1536,640]{1,0:T(8,128)(2,1)} %bitcast.15), custom_call_target="tpu_custom_call" | custom-call | tf_op jit(solution)/shard_map/pallas_call | solution.py:227
  175.4 0.0 copy-start.1
  175.4 3.1 %copy.11 = bf16[1,640,1536]{2,1,0:T(8,128)(2,1)} copy(bf16[1,640,1536]{2,1,0:T(8,128)(2,1)} %bitcast.12) | data formatting | bytes 3932160
  178.5 0.0 copy-done.1
  178.5 0.0 copy-start
  178.5 1.3 copy.12
  179.8 1.0 copy-done
  180.8 1.3 copy.13
Async XLA Ops:
  175.4 3.1 %copy-start.1 = (bf16[640,1536]{1,0:T(8,128)(2,1)S(1)}, bf16[640,1536]{1,0:T(8,128)(2,1)}, u32[]{:S(2)}) copy-start(bf16[640,1536]{1,0:T(8,128)(2,1)} %get-tuple-element.7) | copy-start | bytes 5898244
  178.5 2.3 %copy-start = (bf16[1536,640]{1,0:T(8,128)(2,1)S(1)}, bf16[1536,640]{1,0:T(8,128)(2,1)}, u32[]{:S(2)}) copy-start(bf16[1536,640]{1,0:T(8,128)(2,1)} %get-tuple-element.8) | copy-start | bytes 5898244
where the time goes:
time: 182 us
  Pallas kernels  175 us (96%)
  local copies, waits for them, and re-layouts  6.61 us (4%)
    pallas_call x1, Pallas kernels, step(): pl.pallas_call(functools.partial(kernel, stages, micro, tokens), out_shap...  175 us
    unnamed x7, local copies, waits for them, and re-layouts  6.61 us

commit v1 on v0

v1 whole, which is shorter than its diff:
```python
import functools

import jax
import jax.numpy as jnp
from jax import lax
from jax.experimental import pallas as pl
from jax.experimental.pallas import tpu as pltpu
from jax.sharding import PartitionSpec as P

MESH = pl.DeviceIdType.MESH
CHUNK = 128
BLOCK = 512
LAG = 4
SLOTS = 4

f32, bf16 = jnp.float32, jnp.bfloat16


def dot(a, b):
    return jnp.dot(a, b, preferred_element_type=f32)


def normed(h):
    wide = h.astype(f32)
    scale = lax.rsqrt(jnp.mean(wide * wide, -1, keepdims=True) + 1e-6)
    return wide, scale, (wide * scale).astype(bf16)


def kernel(stages, micro, tokens, x, dy, wg_in, wu_in, wd_in, sum_g, sum_u, sum_d, wg, wu, wd, wgt, wut, wdt, h_in, g_in,
           h_out, g_out, kept_g, kept_u, mid, act, dgate, dup, at, load_sem, h_recv, g_recv, h_send, g_send):
    me = lax.axis_index("pp")
    c, per = CHUNK, tokens // CHUNK
    chunks = micro * per
    ff, d = wd.shape
    ring = kept_g.shape[0]
    columns = [slice(n, n + BLOCK) for n in range(0, ff, BLOCK)]

    loads = [pltpu.make_async_copy(src, dst, load_sem.at[n]) for n, (src, dst) in enumerate(((wg_in, wg), (wu_in, wu), (wd_in, wd)))]
    for load in loads:
        load.start()

    def rows(i):
        return pl.ds(pl.multiple_of(i * c, c), c)

    def fetch(src, dst, sem):
        def one(i, carry):
            pltpu.make_async_copy(src.at[rows(i), :], dst.at[rows(i), :], sem.at[i]).start()
            return carry
        lax.fori_loop(0, chunks, one, 0)

    @pl.when(me == 0)
    def _():
        fetch(x, h_in, h_recv)

    @pl.when(me == stages - 1)
    def _():
        fetch(dy, g_in, g_recv)

    barrier = pltpu.get_barrier_semaphore()

    @pl.when(me > 0)
    def _():
        pl.semaphore_signal(barrier, inc=1, device_id={"pp": me - 1}, device_id_type=MESH)

    @pl.when(me < stages - 1)
    def _():
        pl.semaphore_signal(barrier, inc=1, device_id={"pp": me + 1}, device_id_type=MESH)

    pl.semaphore_wait(barrier, (me > 0).astype(jnp.int32) + (me < stages - 1).astype(jnp.int32))
    for load in loads:
        load.wait()

    def transposes():
        for n in range(0, ff, 256):
            s = slice(n, n + 256)
            wgt[s, :] = wg[:, s].T
            wut[s, :] = wu[:, s].T
            wdt[:, s] = wd[s, :].T

    def h_copy(i):
        return pltpu.make_async_remote_copy(
            src_ref=h_out.at[lax.rem(i, SLOTS)], dst_ref=h_in.at[rows(i), :], send_sem=h_send.at[lax.rem(i, SLOTS)], recv_sem=h_recv.at[i],
            device_id={"pp": me + 1}, device_id_type=MESH)

    def g_copy(i):
        return pltpu.make_async_remote_copy(
            src_ref=g_out.at[lax.rem(i, SLOTS)], dst_ref=g_in.at[rows(i), :], send_sem=g_send.at[lax.rem(i, SLOTS)], recv_sem=g_recv.at[i],
            device_id={"pp": me - 1}, device_id_type=MESH)

    def h_wait(i):
        pltpu.make_async_copy(h_in.at[rows(i), :], h_in.at[rows(i), :], h_recv.at[i]).wait()

    def g_wait(i):
        pltpu.make_async_copy(g_in.at[rows(i), :], g_in.at[rows(i), :], g_recv.at[i]).wait()

    def pieces(i):
        m, q = i // per - 1, lax.rem(i, per)
        half = pl.ds(pl.multiple_of(lax.rem(m, 2) * tokens, tokens), tokens)
        side = lax.rem(m, 2)
        whole = pl.ds(pl.multiple_of(m * tokens, tokens), tokens)

        def add(total, here, s, left, right):
            term = dot(left, right).astype(bf16).astype(f32)
            total[here, s] = jnp.where(m == 0, 0.0, total[here, s]) + term

        share = d // per
        here = pl.ds(pl.multiple_of(q * share, share), share)

        def gate_up(total, by, s):
            add(total, here, s, at[side, here, :], by[half, s])

        def down(n, size):
            there = pl.ds(pl.multiple_of(q * (ff // per) + n, 128), size)
            add(sum_d, there, slice(None), act[half, there].T, g_in[whole, :])

        work = [functools.partial(gate_up, total, by, s) for total, by in ((sum_g, dgate), (sum_u, dup)) for s in columns]
        return work + [functools.partial(down, n, 128) for n in range(0, ff // per, 128)]

    def do(work):
        for piece in work:
            piece()

    def expand(i, a, s, slot):
        gate, up = dot(a, wg[:, s]), dot(a, wu[:, s])
        kept_g[slot, :, s] = gate
        kept_u[slot, :, s] = up
        return gate, up

    def forward(i, role, work):
        h_wait(i)

        @pl.when(i >= SLOTS)
        def _():
            h_copy(i - SLOTS).wait_send()

        do(work[:1])
        a = normed(h_in[rows(i), :])[2]
        for s in columns:
            gate, up = dot(a, wg[:, s]), dot(a, wu[:, s])
            if role == "middle":
                kept_g[lax.rem(i, ring), :, s] = gate
                kept_u[lax.rem(i, ring), :, s] = up
            mid[:, s] = (gate * jax.nn.sigmoid(gate) * up).astype(bf16)
        do(work[1:3])
        m = dot(mid[...], wd[...]).astype(bf16)
        do(work[3:])
        h_out[lax.rem(i, SLOTS)] = (h_in[rows(i), :].astype(f32) + m.astype(f32)).astype(bf16)
        h_copy(i).start()

    def backward(i, role, work):
        if role == "last":
            h_wait(i)
        g_wait(i)
        if role != "first":
            @pl.when(i >= SLOTS)
            def _():
                g_copy(i - SLOTS).wait_send()
        place = lax.rem(i, 2 * per)
        here = pl.ds(pl.multiple_of(place * c, c), c)
        do(work[:1])
        wide, scale, a = normed(h_in[rows(i), :])
        at[lax.rem(i // per, 2), :, pl.ds(pl.multiple_of(lax.rem(i, per) * c, c), c)] = a.T
        g = g_in[rows(i), :]
        for s in columns:
            if role == "middle":
                gate, up = kept_g[lax.rem(i, ring), :, s], kept_u[lax.rem(i, ring), :, s]
            else:
                gate, up = dot(a, wg[:, s]), dot(a, wu[:, s])
            by_act = dot(g, wdt[:, s]).astype(bf16).astype(f32)
            part = jax.nn.sigmoid(gate)
            silu = gate * part
            act[here, s] = (silu * up).astype(bf16)
            dup[here, s] = (by_act * silu).astype(bf16)
            dgate[here, s] = (by_act * up * (part + silu * (1.0 - part))).astype(bf16)
        if role == "first":
            do(work[1:])
            return
        do(work[1:3])
        by_a = dot(dgate[here, :], wgt[...]).astype(bf16).astype(f32) + dot(dup[here, :], wut[...]).astype(bf16).astype(f32)
        do(work[3:])
        by_a = by_a.astype(bf16).astype(f32)
        by_scale = jnp.sum(by_a * wide, -1, keepdims=True)
        by_h = by_a * scale - wide * (by_scale * scale * scale * scale * (1.0 / d))
        g_out[lax.rem(i, SLOTS)] = (g_in[rows(i), :].astype(f32) + by_h.astype(bf16).astype(f32)).astype(bf16)
        g_copy(i).start()

    def loop(start, stop, body):
        def one(t, carry):
            body(t)
            return carry
        lax.fori_loop(start, stop, one, 0)

    def run(role):
        lag = (stages - 1 - me) * LAG

        def step(t):
            i = t - lag
            steady = (t >= lag + per) & (t < chunks)

            @pl.when(steady)
            def _():
                work = pieces(i)
                if role == "last":
                    backward(i, role, [])
                    do(work)
                else:
                    forward(t, role, work[:4])
                    backward(i, role, work[4:])

            if role != "last":
                @pl.when((t < chunks) & ~steady)
                def _():
                    forward(t, role, [])

            if role == "first":
                pl.when(t == SLOTS - 1)(transposes)

            @pl.when((i >= 0) & (i < chunks) & ~steady)
            def _():
                backward(i, role, [])

            @pl.when((i >= per) & ~steady)
            def _():
                do(pieces(i))

        if role != "first":
            transposes()
        loop(0, lag + chunks + per, step)
        for i in range(chunks - SLOTS, chunks):
            if role != "last":
                h_copy(i).wait_send()
            if role != "first":
                g_copy(i).wait_send()

    @pl.when(me == 0)
    def _():
        run("first")

    @pl.when((me > 0) & (me < stages - 1))
    def _():
        run("middle")

    @pl.when(me == stages - 1)
    def _():
        run("last")


def finish(sum_g, sum_u, sum_d, og, ou, od, by_g, by_u, by_d, sem):
    stores = []
    for n, (total, staged, out) in enumerate(((sum_g, by_g, og), (sum_u, by_u, ou), (sum_d, by_d, od))):
        size = total.shape[0] // 4
        for part in range(4):
            here = pl.ds(part * size, size)
            staged[here, :] = total[here, :].astype(bf16)
            stores.append(pltpu.make_async_copy(staged.at[here, :], out.at[here, :], sem.at[n * 4 + part]))
            stores[-1].start()
    for store in stores:
        store.wait()


def solution(mesh):
    stages = mesh.shape["pp"]

    def step(x, dy, w_gate, w_up, w_down):
        micro, tokens, d = x.shape
        ff = w_gate.shape[-1]
        chunks = micro * tokens // CHUNK
        ring = (stages - 2) * LAG + 1
        hbm = pl.BlockSpec(memory_space=pl.ANY)
        dma = pltpu.SemaphoreType.DMA
        shapes = [w.shape[1:] for w in (w_gate, w_up, w_down)]
        sums = pl.pallas_call(
            functools.partial(kernel, stages, micro, tokens),
            out_shape=[pltpu.VMEM(shape, f32) for shape in shapes],
            in_specs=[hbm] * 5,
            out_specs=[pl.BlockSpec(memory_space=pltpu.VMEM)] * 3,
            scratch_shapes=[
                pltpu.VMEM((d, ff), bf16), pltpu.VMEM((d, ff), bf16), pltpu.VMEM((ff, d), bf16),
                pltpu.VMEM((ff, d), bf16), pltpu.VMEM((ff, d), bf16), pltpu.VMEM((d, ff), bf16),
                pltpu.VMEM((micro * tokens, d), bf16), pltpu.VMEM((micro * tokens, d), bf16),
                pltpu.VMEM((SLOTS, CHUNK, d), bf16), pltpu.VMEM((SLOTS, CHUNK, d), bf16),
                pltpu.VMEM((ring, CHUNK, ff), f32), pltpu.VMEM((ring, CHUNK, ff), f32),
                pltpu.VMEM((CHUNK, ff), bf16),
                pltpu.VMEM((2 * tokens, ff), bf16), pltpu.VMEM((2 * tokens, ff), bf16), pltpu.VMEM((2 * tokens, ff), bf16),
                pltpu.VMEM((2, d, tokens), bf16),
                dma((3,)), dma((chunks,)), dma((chunks,)), dma((SLOTS,)), dma((SLOTS,)),
            ],
            compiler_params=pltpu.CompilerParams(collective_id=0, has_side_effects=True, vmem_limit_bytes=50 * 2**20),
        )(x.reshape(micro * tokens, d), dy.reshape(micro * tokens, d), w_gate[0], w_up[0], w_down[0])
        outs = pl.pallas_call(
            finish,
            out_shape=[jax.ShapeDtypeStruct(shape, bf16) for shape in shapes],
            in_specs=[pl.BlockSpec(memory_space=pltpu.VMEM)] * 3,
            out_specs=[hbm] * 3,
            scratch_shapes=[pltpu.VMEM(shape, bf16) for shape in shapes] + [dma((12,))],
            compiler_params=pltpu.CompilerParams(vmem_limit_bytes=16 * 2**20),
        )(*sums)
        return tuple(out[None] for out in outs)

    return jax.shard_map(
        step,
        mesh=mesh,
        in_specs=(P("rep", None, None),) * 2 + (P("pp", None, None),) * 3,
        out_specs=(P(("rep", "pp"), None, None),) * 3,
        check_vma=False,
    )
```

time: 182 us -> 167 us (0.918)
  Pallas kernels: 175 us -> 166 us
  local copies, waits for them, and re-layouts: 6.61 us -> 0 us
    pallas_call x1, Pallas kernels: 175 us -> 164 us  [step(): pl.pallas_call(functools.partial(kernel, stages, micro, tokens), out_shap...]
    unnamed x7 -> x0, local copies, waits for them, and re-layouts: 6.61 us -> none
    pallas_call x0 -> x1, Pallas kernels: none -> 2.69 us  [step(): pl.pallas_call(finish, out_shape=[jax.ShapeDtypeStruct(shape, bf16) for s...]
where the time goes in v1:
time: 167 us
  Pallas kernels  166 us (99%)
    pallas_call x1, Pallas kernels, step(): pl.pallas_call(functools.partial(kernel, stages, micro, tokens), out_shap...  164 us

profile of v1, /device:TPU:120, one launch (start us, length us, event | category | flops | bytes accessed | tf_op | source)
XLA Modules:
  0.0 167.3 jit_solution(7596551765551016354)
XLA Ops:
  0.6 163.8 %shard_map.76 = (f32[640,1536]{1,0:T(8,128)S(1)}, f32[640,1536]{1,0:T(8,128)S(1)}, f32[1536,640]{1,0:T(8,128)S(1)}) custom-call(bf16[4096,640]{1,0:T(8,128)(2,1)} %bitcast.8, bf16[4096,640]{1,0:T(8,128)(2,1)} %bitcast.9, bf16[640,1536]{1,0:T(8,128)(2,1)} %bitcast.10, bf16[640,1536]{1,0:T(8,128)(2,1)} %bitcast.11, bf16[1536,640]{1,0:T(8,128)(2,1)} %bitcast.12), custom_call_target="tpu_custom_call" | custom-call | tf_op jit(solution)/shard_map/pallas_call | solution.py:272
  164.4 2.7 %shard_map.77 = (bf16[640,1536]{1,0:T(8,128)(2,1)}, bf16[640,1536]{1,0:T(8,128)(2,1)}, bf16[1536,640]{1,0:T(8,128)(2,1)}) custom-call(f32[640,1536]{1,0:T(8,128)S(1)} %get-tuple-element.9.sum_g, f32[640,1536]{1,0:T(8,128)S(1)} %get-tuple-element.10.sum_u, f32[1536,640]{1,0:T(8,128)S(1)} %get-tuple-element.11.sum_d), custom_call_target="tpu_custom_call" | custom-call | tf_op jit(solution)/shard_map/pallas_call | solution.py:290

commit v2 on v1

v2 whole, which is shorter than its diff:
```python
import functools

import jax
import jax.numpy as jnp
from jax import lax
from jax.experimental import pallas as pl
from jax.experimental.pallas import tpu as pltpu
from jax.sharding import PartitionSpec as P

MESH = pl.DeviceIdType.MESH
CHUNK = 128
BLOCK = 512
ENDS = 2
LAG = 4
SLOTS = 3

f32, bf16 = jnp.float32, jnp.bfloat16


def dot(a, b):
    return jnp.dot(a, b, preferred_element_type=f32)


def normed(h):
    wide = h.astype(f32)
    scale = lax.rsqrt(jnp.mean(wide * wide, -1, keepdims=True) + 1e-6)
    return wide, scale, (wide * scale).astype(bf16)


def kernel(stages, micro, tokens, x, dy, wg_in, wu_in, wd_in, sum_g, sum_u, sum_d, wg, wu, wd, wgt, wut, wdt, h_in, g_in,
           h_out, g_out, kept_g, kept_u, mid, act, dgate, dup, new_dgate, new_dup, at, load_sem, h_recv, g_recv, h_send, g_send):
    me = lax.axis_index("pp")
    c, per, small = CHUNK, tokens // CHUNK, CHUNK // ENDS
    chunks = micro * per
    items = chunks - 2 + 2 * ENDS
    tail = items - ENDS
    ff, d = wd.shape
    ring = kept_g.shape[0]
    new_by, new_act = mid.at[0], mid.at[1]
    columns = [slice(n, n + BLOCK) for n in range(0, ff, BLOCK)]

    def begin(i):
        return jnp.where(i < ENDS, i * small, jnp.where(i < tail, (i - ENDS + 1) * c, (chunks - 1) * c + (i - tail) * small))

    def rows(i, size):
        return pl.ds(pl.multiple_of(begin(i), small), size)

    def whole(i):
        return (i >= ENDS) & (i < tail)

    def fetch(src, dst, sem, since, until):
        for start, stop, size in ((0, ENDS, small), (ENDS, tail, c), (tail, items, small)):
            if not since <= start < until:
                continue

            def one(i, carry):
                pltpu.make_async_copy(src.at[rows(i, size), :], dst.at[rows(i, size), :], sem.at[i]).start()
                return carry
            lax.fori_loop(start, stop, one, 0)

    @pl.when(me == 0)
    def _():
        fetch(x, h_in, h_recv, 0, ENDS)

    @pl.when(me == stages - 1)
    def _():
        fetch(dy, g_in, g_recv, 0, ENDS)

    loads = [pltpu.make_async_copy(src, dst, load_sem.at[n]) for n, (src, dst) in enumerate(((wg_in, wg), (wu_in, wu), (wd_in, wd)))]
    for load in loads:
        load.start()

    @pl.when(me == 0)
    def _():
        fetch(x, h_in, h_recv, ENDS, items)

    @pl.when(me == stages - 1)
    def _():
        fetch(dy, g_in, g_recv, ENDS, items)

    barrier = pltpu.get_barrier_semaphore()

    @pl.when(me > 0)
    def _():
        pl.semaphore_signal(barrier, inc=1, device_id={"pp": me - 1}, device_id_type=MESH)

    @pl.when(me < stages - 1)
    def _():
        pl.semaphore_signal(barrier, inc=1, device_id={"pp": me + 1}, device_id_type=MESH)

    pl.semaphore_wait(barrier, (me > 0).astype(jnp.int32) + (me < stages - 1).astype(jnp.int32))
    for load in loads:
        load.wait()

    def prepare():
        for n in range(0, ff, 256):
            s = slice(n, n + 256)
            wgt[s, :] = wg[:, s].T
            wut[s, :] = wu[:, s].T
            wdt[:, s] = wd[s, :].T
        for total in (sum_g, sum_u, sum_d):
            total[...] = jnp.zeros_like(total)

    def h_copy(i, size):
        slot = lax.rem(i, SLOTS)
        return pltpu.make_async_remote_copy(
            src_ref=h_out.at[slot, pl.ds(0, size), :], dst_ref=h_in.at[rows(i, size), :], send_sem=h_send.at[slot], recv_sem=h_recv.at[i],
            device_id={"pp": me + 1}, device_id_type=MESH)

    def g_copy(i, size):
        slot = lax.rem(i, SLOTS)
        return pltpu.make_async_remote_copy(
            src_ref=g_out.at[slot, pl.ds(0, size), :], dst_ref=g_in.at[rows(i, size), :], send_sem=g_send.at[slot], recv_sem=g_recv.at[i],
            device_id={"pp": me - 1}, device_id_type=MESH)

    def sent(copy, i):
        @pl.when((i >= 0) & whole(i))
        def _():
            copy(i, c).wait_send()

        @pl.when((i >= 0) & ~whole(i))
        def _():
            copy(i, small).wait_send()

    def h_wait(i, size):
        pltpu.make_async_copy(h_in.at[rows(i, size), :], h_in.at[rows(i, size), :], h_recv.at[i]).wait()

    def g_wait(i, size):
        pltpu.make_async_copy(g_in.at[rows(i, size), :], g_in.at[rows(i, size), :], g_recv.at[i]).wait()

    def pieces(i):
        m, q = i // per - 1, lax.rem(i, per)
        half = pl.ds(pl.multiple_of(lax.rem(m, 2) * tokens, tokens), tokens)
        side = lax.rem(m, 2)
        batch = pl.ds(pl.multiple_of(m * tokens, tokens), tokens)

        def add(total, here, s, left, right):
            term = dot(left, right).astype(bf16).astype(f32)
            total[here, s] += term

        share = d // per
        here = pl.ds(pl.multiple_of(q * share, share), share)

        def gate_up(total, by, s):
            add(total, here, s, at[side, here, :], by[half, s])

        def down(n, size):
            there = pl.ds(pl.multiple_of(q * (ff // per) + n, 128), size)
            add(sum_d, there, slice(None), act[half, there].T, g_in[batch, :])

        work = [functools.partial(gate_up, total, by, s) for total, by in ((sum_g, dgate), (sum_u, dup)) for s in columns]
        return work + [functools.partial(down, n, 128) for n in range(0, ff // per, 128)]

    def do(work):
        for piece in work:
            piece()

    def expand(i, a, s, slot):
        gate, up = dot(a, wg[:, s]), dot(a, wu[:, s])
        kept_g[slot, :, s] = gate
        kept_u[slot, :, s] = up
        return gate, up

    def expand(a, s, out):
        gate, up = dot(a, wg[:, s]), dot(a, wu[:, s])
        part = jax.nn.sigmoid(gate)
        silu = gate * part
        out[:, s] = (silu * up).astype(bf16)
        return up * (part + silu * (1.0 - part)), silu

    def place(i, size):
        return pl.ds(pl.multiple_of(lax.rem(begin(i), 2 * tokens), size), size)

    def forward(i, size, role, head=(), tail=()):
        h_wait(i, size)
        sent(h_copy, i - SLOTS)
        slot = lax.rem(i, ring) if role == "middle" else 0
        do(head)
        a = normed(h_in[rows(i, size), :])[2]
        for s in columns:
            to_gate, to_up = expand(a, s, mid.at[slot, pl.ds(0, size), :])
            if role == "middle":
                kept_g[slot, :size, s] = to_gate
                kept_u[slot, :size, s] = to_up
        m = dot(mid[slot, :size, :], wd[...]).astype(bf16)
        do(tail)
        h_out[lax.rem(i, SLOTS), :size] = (h_in[rows(i, size), :].astype(f32) + m.astype(f32)).astype(bf16)
        h_copy(i, size).start()

    def keep(a, start):
        at[lax.rem(start // tokens, 2), :, pl.ds(pl.multiple_of(lax.rem(start, tokens), c), c)] = a.T

    def again(i, size):
        a = normed(h_in[rows(i, size), :])[2]
        for s in columns:
            kept_g[0, :size, s], kept_u[0, :size, s] = expand(a, s, new_act.at[pl.ds(0, size), :])
        if size == c:
            keep(a, begin(i))

    def backward(i, size, role, head=(), tail=()):
        here, slot = place(i, size), lax.rem(i, ring) if role == "middle" else 0
        if role == "middle":
            if size == c:
                keep(normed(h_in[rows(i, size), :])[2], begin(i))
            act[here, :] = mid[slot, :size, :]
        g_wait(i, size)
        if role != "first":
            sent(g_copy, i - SLOTS)
        if role == "last":
            new_by[:size, :] = dot(g_in[rows(i, size), :], wdt[...]).astype(bf16)
            h_wait(i, size)
        if role != "first":
            wide, scale, a = normed(h_in[rows(i, size), :])
        if role == "last" and size == c:
            keep(a, begin(i))

        def store():
            if role != "middle":
                act[here, :] = new_act[:size, :]
            dup[here, :] = new_dup[:size, :]
            dgate[here, :] = new_dgate[:size, :]

        g = g_in[rows(i, size), :]
        for s in columns:
            by_act = new_by[:size, s] if role == "last" else dot(g, wdt[:, s]).astype(bf16)
            by_act = by_act.astype(f32)
            if role == "last":
                to_gate, to_up = expand(a, s, new_act.at[pl.ds(0, size), :])
            else:
                to_gate, to_up = kept_g[slot, :size, s], kept_u[slot, :size, s]
            new_dup[:size, s] = (by_act * to_up).astype(bf16)
            new_dgate[:size, s] = (by_act * to_gate).astype(bf16)
        do(head)
        if role != "first":
            by_a = dot(new_dgate[:size, :], wgt[...]).astype(bf16).astype(f32) + dot(new_dup[:size, :], wut[...]).astype(bf16).astype(f32)
            do(tail)
            store()
            by_a = by_a.astype(bf16).astype(f32)
            by_scale = jnp.sum(by_a * wide, -1, keepdims=True)
            by_h = by_a * scale - wide * (by_scale * scale * scale * scale * (1.0 / d))
            g_out[lax.rem(i, SLOTS), :size] = (g_in[rows(i, size), :].astype(f32) + by_h.astype(bf16).astype(f32)).astype(bf16)
            g_copy(i, size).start()
        else:
            do(tail)
            store()
        if size != c:
            @pl.when((i == ENDS - 1) | (i == items - 1))
            def _():
                first = begin(i) - (ENDS - 1) * small
                keep(normed(h_in[pl.ds(pl.multiple_of(first, c), c), :])[2], first)

    def loop(start, stop, body):
        def one(t, carry):
            body(t)
            return carry
        lax.fori_loop(start, stop, one, 0)

    def run(role):
        lag = jnp.where(me < stages - 1, LAG * (stages - 1 - me) - 1, 0)

        def share(i):
            return jnp.where(i < items, i - ENDS + 1, i - items + chunks)

        def step(t):
            i = t - lag
            steady = whole(t) & (i >= per + ENDS - 1) & (i < tail)

            @pl.when(steady)
            def _():
                work = pieces(share(i))
                if role == "last":
                    backward(i, c, role)
                    do(work)
                elif role == "middle":
                    forward(t, c, role)
                    do(work)
                    backward(i, c, role)
                else:
                    forward(t, c, role, work[:1], [functools.partial(again, i, c)] + work[1:2])
                    backward(i, c, role, work[2:4], work[4:])

            @pl.when(~steady)
            def _():
                for size, right in ((c, whole), (small, lambda i: ~whole(i))):
                    if role != "last":
                        @pl.when((t < items) & right(t))
                        def _():
                            forward(t, size, role)

                if role == "first":
                    pl.when(t == ENDS + 1)(prepare)

                for size, right in ((c, whole), (small, lambda i: ~whole(i))):
                    @pl.when((i >= 0) & (i < items) & right(i))
                    def _():
                        if role == "first":
                            again(i, size)
                        backward(i, size, role)

                @pl.when((i >= per + ENDS - 1) & (i <= tail) | (i >= items))
                def _():
                    do(pieces(share(i)))

        if role != "first":
            prepare()
        loop(0, lag + items + per, step)
        for i in range(items - SLOTS, items):
            if role != "last":
                sent(h_copy, i)
            if role != "first":
                sent(g_copy, i)

    @pl.when(me == 0)
    def _():
        run("first")

    @pl.when((me > 0) & (me < stages - 1))
    def _():
        run("middle")

    @pl.when(me == stages - 1)
    def _():
        run("last")


def finish(sum_g, sum_u, sum_d, og, ou, od, by_g, by_u, by_d, sem):
    stores = []
    for n, (total, staged, out) in enumerate(((sum_g, by_g, og), (sum_u, by_u, ou), (sum_d, by_d, od))):
        size = total.shape[0] // 4
        for part in range(4):
            here = pl.ds(part * size, size)
            staged[here, :] = total[here, :].astype(bf16)
            stores.append(pltpu.make_async_copy(staged.at[here, :], out.at[here, :], sem.at[n * 4 + part]))
            stores[-1].start()
    for store in stores:
        store.wait()


def solution(mesh):
    stages = mesh.shape["pp"]

    def step(x, dy, w_gate, w_up, w_down):
        micro, tokens, d = x.shape
        ff = w_gate.shape[-1]
        items = micro * tokens // CHUNK - 2 + 2 * ENDS
        ring = (stages - 2) * LAG
        hbm = pl.BlockSpec(memory_space=pl.ANY)
        dma = pltpu.SemaphoreType.DMA
        shapes = [w.shape[1:] for w in (w_gate, w_up, w_down)]
        sums = pl.pallas_call(
            functools.partial(kernel, stages, micro, tokens),
            out_shape=[pltpu.VMEM(shape, f32) for shape in shapes],
            in_specs=[hbm] * 5,
            out_specs=[pl.BlockSpec(memory_space=pltpu.VMEM)] * 3,
            scratch_shapes=[
                pltpu.VMEM((d, ff), bf16), pltpu.VMEM((d, ff), bf16), pltpu.VMEM((ff, d), bf16),
                pltpu.VMEM((ff, d), bf16), pltpu.VMEM((ff, d), bf16), pltpu.VMEM((d, ff), bf16),
                pltpu.VMEM((micro * tokens, d), bf16), pltpu.VMEM((micro * tokens, d), bf16),
                pltpu.VMEM((SLOTS, CHUNK, d), bf16), pltpu.VMEM((SLOTS, CHUNK, d), bf16),
                pltpu.VMEM((ring, CHUNK, ff), f32), pltpu.VMEM((ring, CHUNK, ff), f32),
                pltpu.VMEM((ring, CHUNK, ff), bf16),
                pltpu.VMEM((2 * tokens, ff), bf16), pltpu.VMEM((2 * tokens, ff), bf16), pltpu.VMEM((2 * tokens, ff), bf16),
                pltpu.VMEM((CHUNK, ff), bf16), pltpu.VMEM((CHUNK, ff), bf16),
                pltpu.VMEM((2, d, tokens), bf16),
                dma((3,)), dma((items,)), dma((items,)), dma((SLOTS,)), dma((SLOTS,)),
            ],
            compiler_params=pltpu.CompilerParams(collective_id=0, has_side_effects=True, vmem_limit_bytes=int(52.5 * 2**20)),
        )(x.reshape(micro * tokens, d), dy.reshape(micro * tokens, d), w_gate[0], w_up[0], w_down[0])
        outs = pl.pallas_call(
            finish,
            out_shape=[jax.ShapeDtypeStruct(shape, bf16) for shape in shapes],
            in_specs=[pl.BlockSpec(memory_space=pltpu.VMEM)] * 3,
            out_specs=[hbm] * 3,
            scratch_shapes=[pltpu.VMEM(shape, bf16) for shape in shapes] + [dma((12,))],
            compiler_params=pltpu.CompilerParams(vmem_limit_bytes=16 * 2**20),
        )(*sums)
        return tuple(out[None] for out in outs)

    return jax.shard_map(
        step,
        mesh=mesh,
        in_specs=(P("rep", None, None),) * 2 + (P("pp", None, None),) * 3,
        out_specs=(P(("rep", "pp"), None, None),) * 3,
        check_vma=False,
    )
```

time: 167 us -> 167 us (level)
  no operation moved by 1% of the time
where the time goes in v2:
time: 167 us
  Pallas kernels  166 us (99%)
    pallas_call x1, Pallas kernels, step(): pl.pallas_call(functools.partial(kernel, stages, micro, tokens), out_shap...  163 us

profile of v2, /device:TPU:120, one launch (start us, length us, event | category | flops | bytes accessed | tf_op | source)
XLA Modules:
  0.0 166.6 jit_solution(12446856220228566063)
XLA Ops:
  0.6 163.1 %shard_map.76 = (f32[640,1536]{1,0:T(8,128)S(1)}, f32[640,1536]{1,0:T(8,128)S(1)}, f32[1536,640]{1,0:T(8,128)S(1)}) custom-call(bf16[4096,640]{1,0:T(8,128)(2,1)} %bitcast.8, bf16[4096,640]{1,0:T(8,128)(2,1)} %bitcast.9, bf16[640,1536]{1,0:T(8,128)(2,1)} %bitcast.10, bf16[640,1536]{1,0:T(8,128)(2,1)} %bitcast.11, bf16[1536,640]{1,0:T(8,128)(2,1)} %bitcast.12), custom_call_target="tpu_custom_call" | custom-call | tf_op jit(solution)/shard_map/pallas_call | solution.py:350
  163.7 2.7 %shard_map.77 = (bf16[640,1536]{1,0:T(8,128)(2,1)}, bf16[640,1536]{1,0:T(8,128)(2,1)}, bf16[1536,640]{1,0:T(8,128)(2,1)}) custom-call(f32[640,1536]{1,0:T(8,128)S(1)} %get-tuple-element.9.sum_g, f32[640,1536]{1,0:T(8,128)S(1)} %get-tuple-element.10.sum_u, f32[1536,640]{1,0:T(8,128)S(1)} %get-tuple-element.11.sum_d), custom_call_target="tpu_custom_call" | custom-call | tf_op jit(solution)/shard_map/pallas_call | solution.py:369
